TPU v7x, 256 devices: a whole 4x4x8 slice. The times are simulated.
256 devices in a mesh: section: 2 (over y_hi), pen: 64 (over y_lo, z, x), slab: 2 (over core).
Axes of the slice: x: 4, y: 4 (y_hi: 2, y_lo: 2; y = y_hi * 2 + y_lo), z: 8, core: 2. Of those that a mesh axis runs over, the one named last changes fastest.
Arguments:
- velocity: float32 [3, 384, 384, 384], P(None, ('section', 'pen'), 'slab'), may hold values from -6 to 6
- vorticity: float32 [3, 384, 384, 384], P(None, ('section', 'pen'), 'slab'), may hold values from -6 to 6
- velocity_modes: float32 [3, 256, 256, 2, 256], P(None, None, ('section', 'pen'), None, 'slab'), may hold values from -6 to 6
Outputs:
- rhs_modes: float32 [3, 256, 256, 2, 256], P(None, None, ('section', 'pen'), None, 'slab')
All inputs are finite; a program needn't handle non-finite values.
Results may differ from a plain program's by a relative error of at most 0.000057.
Values sent between devices are 32-bit elements; how exact they have to be, the bound alone decides.
A program may use at most 64 MiB of HBM per device.

v0:
```python
import functools
import math

import jax
import jax.numpy as jnp
import numpy as np
from jax import lax
from jax.experimental import pallas as pl
from jax.experimental.pallas import tpu as pltpu
from jax.sharding import PartitionSpec as P

MESH = pl.DeviceIdType.MESH
f32, bf16 = jnp.float32, jnp.bfloat16


def signed(count):
    j = np.arange(count)
    return np.where(j < count // 2, j, j - count)


def high_low(table):
    high = table.astype(np.float32).astype(bf16)
    low = (table - high.astype(np.float64)).astype(np.float32).astype(bf16)
    return high, low


def tables(n, keep, devices):
    k = signed(keep)
    phase = 2.0 * math.pi / n * np.mod(k[:, None] * np.arange(n)[None, :], n)
    cos, sin = np.cos(phase) / math.sqrt(n), np.sin(phase) / math.sqrt(n)
    half = keep // 2
    tx = []
    for b in range(2):
        rows = slice(b * half, (b + 1) * half)
        high, low = high_low(np.concatenate([cos[rows].T, -sin[rows].T], axis=1))
        tx.append(np.concatenate([high, low, high], axis=0))
    ty = []
    for p in range(2):
        high, low = high_low(np.concatenate([cos[p::2, : n // 2], sin[p::2, : n // 2]], axis=0))
        ty.append(np.concatenate([high, low, high], axis=1))
    order = np.arange(n).reshape(devices, n // devices).T.reshape(-1)
    high, low = high_low(np.concatenate([cos[:, order], sin[:, order]], axis=0))
    tz = np.concatenate([high, low, high], axis=1)
    return np.stack(tx), np.stack(ty), tz


def split(x):
    high = x.astype(bf16)
    return high, (x - high.astype(f32)).astype(bf16)


def kernel(
    dims, v_hbm, w_hbm, m_hbm, tx_hbm, ty_hbm, tz_hbm, out,
    v, w, modes, tx, ty, tz, own, away, arrived, outbox, inbox, spec,
    in_sem, m_sem, t_sem, xs_sem, xr_sem, self_sem, s_sem, r_sem,
):
    ny, nz, nx, planes, keep, n = dims
    half = keep // 2
    group = ny * nz * nx
    quad = 4 * planes
    me = lax.axis_index("section") * (group // 2) + lax.axis_index("pen")
    slab = lax.axis_index("slab")
    mx, mz, my = me % nx, (me // nx) % nz, me // (nx * nz)

    def peer(i):
        j = i // (nx * ny)
        rest = i % (nx * ny)
        dz = nz // 2 + ((j + 1) // 2) * (2 * (j % 2) - 1)
        dy = ny // 2 + rest // nx
        dx = nx // 2 + rest % nx
        return ((my + dy) % ny) * (nx * nz) + ((mz + dz) % nz) * nx + (mx + dx) % nx

    def device(t, s):
        return {"section": t // (group // 2), "pen": t % (group // 2), "slab": s}

    self_step = (nz - 1) * nx * ny + (ny // 2) * nx + nx // 2

    def each_peer(body):
        def step(i, carry):
            body(peer(i + jnp.where(i >= self_step, 1, 0)))
            return carry

        lax.fori_loop(0, group - 1, step, 0)

    barrier = pltpu.get_barrier_semaphore()
    each_peer(
        lambda t: pl.semaphore_signal(barrier, inc=1, device_id=device(t, slab), device_id_type=MESH)
    )
    pl.semaphore_signal(barrier, inc=1, device_id=device(me, 1 - slab), device_id_type=MESH)

    loads = [
        pltpu.make_async_copy(tx_hbm, tx, t_sem.at[0]),
        pltpu.make_async_copy(ty_hbm, ty, t_sem.at[1]),
        pltpu.make_async_copy(tz_hbm, tz, t_sem.at[2]),
    ]
    loads[0].start()
    inputs = {}
    for c in (1, 2, 0):
        for i, (src, dst) in enumerate(((v_hbm, v), (w_hbm, w))):
            inputs[c, i] = pltpu.make_async_copy(src.at[c], dst.at[c], in_sem.at[2 * c + i])
            inputs[c, i].start()
    loads[1].start()
    loads[2].start()
    mode_load = pltpu.make_async_copy(m_hbm, modes, m_sem)
    mode_load.start()

    loads[0].wait()
    for c in range(3):
        a, b = (c + 1) % 3, (c + 2) % 3
        if c == 0:
            for key in ((1, 0), (1, 1), (2, 0), (2, 1)):
                inputs[key].wait()
        if c == 1:
            for key in ((0, 0), (0, 1)):
                inputs[key].wait()

        def x_plane(z, carry, a=a, b=b, c=c):
            p = v[a, z] * w[b, z] - v[b, z] * w[a, z]
            high, low = split(p)
            lhs = jnp.concatenate([high, high, low], axis=1)
            away[c * planes + z] = jnp.dot(lhs, tx[1 - slab], preferred_element_type=f32)
            own[c * planes + z] = jnp.dot(lhs, tx[slab], preferred_element_type=f32)
            return carry

        lax.fori_loop(0, planes, x_plane, 0)

    pl.semaphore_wait(barrier, group)

    def swap(p):
        return pltpu.make_async_remote_copy(
            src_ref=away.at[p],
            dst_ref=arrived.at[p],
            send_sem=xs_sem.at[p],
            recv_sem=xr_sem.at[p],
            device_id=device(me, 1 - slab),
            device_id_type=MESH,
        )

    for p in range(3 * planes):
        swap(p).start()
    loads[1].wait()
    sign = (1 - 2 * slab).astype(f32)

    def component(c, carry):
        def y_plane(z, carry):
            p = c * planes + z
            swap(p).wait_recv()
            mine, other = own[p], arrived[p]
            for parity, folded in enumerate((mine + other, sign * (mine - other))):
                high, low = split(folded)
                both = jnp.dot(
                    ty[parity],
                    jnp.concatenate([high, high, low], axis=0),
                    preferred_element_type=f32,
                )
                row = z * 4 + parity * 2
                outbox[c, pl.ds(row, half, stride=quad), :] = both[:half, :half] + both[half:, half:]
                outbox[c, pl.ds(row + 1, half, stride=quad), :] = (
                    both[:half, half:] - both[half:, :half]
                )
            return carry

        lax.fori_loop(0, planes, y_plane, 0)

        def send(t):
            pltpu.make_async_remote_copy(
                src_ref=outbox.at[c, pl.ds(t * quad, quad)],
                dst_ref=inbox.at[c, pl.ds(me * quad, quad)],
                send_sem=s_sem.at[c],
                recv_sem=r_sem.at[c],
                device_id=device(t, slab),
                device_id_type=MESH,
            ).start()

        each_peer(send)
        pltpu.make_async_copy(
            outbox.at[c, pl.ds(me * quad, quad)], inbox.at[c, pl.ds(me * quad, quad)], self_sem.at[c]
        ).start()
        return carry

    lax.fori_loop(0, 3, component, 0)
    loads[2].wait()

    def z_component(c, carry):
        some = pl.ds(0, (group - 1) * quad)
        pltpu.make_async_copy(outbox.at[c, some], inbox.at[c, some], r_sem.at[c]).wait()
        pltpu.make_async_copy(
            outbox.at[c, pl.ds(me * quad, quad)], inbox.at[c, pl.ds(me * quad, quad)], self_sem.at[c]
        ).wait()
        for q in range(2):
            pieces = [
                jnp.concatenate(
                    [inbox[c, pl.ds(r * 4 + q * 2 + part, group, stride=quad), :] for r in range(planes)],
                    axis=0,
                )
                for part in range(2)
            ]
            high, low = split(jnp.concatenate(pieces, axis=1))
            both = jnp.dot(
                tz[...], jnp.concatenate([high, high, low], axis=0), preferred_element_type=f32
            )
            spec[c, 2 * q] = both[:keep, :half] + both[keep:, half:]
            spec[c, 2 * q + 1] = both[:keep, half:] - both[keep:, :half]
        return carry

    lax.fori_loop(0, 3, z_component, 0)
    mode_load.wait()

    limit = -half
    to_wave = lambda j: jnp.where(j < half, j, j - keep)
    kz = to_wave(lax.broadcasted_iota(jnp.int32, (keep, half), 0))
    kx = to_wave(slab * half + lax.broadcasted_iota(jnp.int32, (keep, half), 1))
    visc = 0.5 / half**2
    for q in range(2):
        ky = jnp.full((keep, half), to_wave(2 * me + q), jnp.int32)
        kept = ((kx != limit) & (ky != limit) & (kz != limit)).astype(f32)
        waves = (kx.astype(f32), ky.astype(f32), kz.astype(f32))
        ksq = waves[0] * waves[0] + waves[1] * waves[1] + waves[2] * waves[2]
        scale = 1.0 / jnp.maximum(ksq, 1.0)
        for part in range(2):
            row = 2 * q + part
            s = [spec[c, row] for c in range(3)]
            inner = (waves[0] * s[0] + waves[1] * s[1] + waves[2] * s[2]) * scale
            for c in range(3):
                rows = pl.ds(row, keep, stride=4)
                out[c, rows, :] = (s[c] - waves[c] * inner) * kept - visc * ksq * modes[c, rows, :]

    for p in range(3 * planes):
        swap(p).wait_send()
    for c in range(3):
        some = pl.ds(0, (group - 1) * quad)
        pltpu.make_async_copy(outbox.at[c, some], inbox.at[c, some], s_sem.at[c]).wait()


def per_device(sizes, velocity, vorticity, velocity_modes):
    ny, nz, nx = sizes
    _, planes, rows, n = velocity.shape
    keep, half = velocity_modes.shape[1], velocity_modes.shape[4]
    group = ny * nz * nx
    tx, ty, tz = tables(n, keep, group)
    anywhere = pl.BlockSpec(memory_space=pl.ANY)
    quad = 4 * planes
    dma = pltpu.SemaphoreType.DMA
    out = pl.pallas_call(
        functools.partial(kernel, (ny, nz, nx, planes, keep, n)),
        out_shape=jax.ShapeDtypeStruct((3, 4 * keep, half), f32),
        in_specs=[anywhere] * 6,
        out_specs=pl.BlockSpec(memory_space=pltpu.VMEM),
        scratch_shapes=[
            pltpu.VMEM((3, planes, rows, n), f32),
            pltpu.VMEM((3, planes, rows, n), f32),
            pltpu.VMEM((3, 4 * keep, half), f32),
            pltpu.VMEM(tx.shape, bf16),
            pltpu.VMEM(ty.shape, bf16),
            pltpu.VMEM(tz.shape, bf16),
            pltpu.VMEM((3 * planes, rows, keep), f32),
            pltpu.VMEM((3 * planes, rows, keep), f32),
            pltpu.VMEM((3 * planes, rows, keep), f32),
            pltpu.VMEM((3, group * quad, half), f32),
            pltpu.VMEM((3, group * quad, half), f32),
            pltpu.VMEM((3, 4, keep, half), f32),
            dma((6,)),
            dma,
            dma((3,)),
            dma((3 * planes,)),
            dma((3 * planes,)),
            dma((3,)),
            dma((3,)),
            dma((3,)),
        ],
        compiler_params=pltpu.CompilerParams(
            collective_id=0, has_side_effects=True, vmem_limit_bytes=60 << 20
        ),
    )(velocity, vorticity, velocity_modes.reshape(3, 4 * keep, half), tx, ty, tz)
    return out.reshape(velocity_modes.shape)


def solution(mesh):
    sizes = (4, 8, 4)
    return jax.shard_map(
        functools.partial(per_device, sizes),
        mesh=mesh,
        in_specs=(
            P(None, ("section", "pen"), "slab", None),
            P(None, ("section", "pen"), "slab", None),
            P(None, None, ("section", "pen"), None, "slab"),
        ),
        out_specs=P(None, None, ("section", "pen"), None, "slab"),
        check_vma=False,
    )
```

profile of v0, /device:TPU:1, one launch (start us, length us, event | category | flops | bytes accessed | tf_op | source)
XLA Modules:
  0.0 84.4 jit_solution(4345331932462701686)
XLA Ops:
  0.0 81.3 %shard_map.64 = f32[3,1024,128]{2,1,0:T(8,128)} custom-call(f32[3,3,192,384]{3,2,1,0:T(8,128)} %v_hbm.1, f32[3,3,192,384]{3,2,1,0:T(8,128)} %w_hbm.1, f32[3,1024,128]{2,1,0:T(8,128)} %bitcast.3, bf16[2,1152,256]{2,1,0:T(8,128)(2,1)} %constant.6.clone.tx_hbm, bf16[2,256,576]{2,1,0:T(8,128)(2,1)} %constant.7.clone.ty_hbm, bf16[512,1152]{1,0:T(8,128)(2,1)} %constant.8.clone.tz_hbm), custom_call_target="tpu_custom_call" | custom-call | tf_op jit(solution)/shard_map/pallas_call | solution.py:244
  81.3 3.1 %copy.8 = f32[3,256,2,2,128]{4,3,2,1,0:T(2,128)} copy(f32[3,256,2,2,128]{4,3,2,1,0:T(2,128)} %bitcast.2) | data formatting | bytes 3145728
where the time goes:
time: 84.5 us; the launch traced here: 84.4 us
  Pallas kernels  81.3 us (96%)
  local copies, waits for them, and re-layouts  3.09 us (4%)
    pallas_call x1, Pallas kernels, per_device(): pl.pallas_call(functools.partial(kernel, (ny, nz, nx, planes, keep, n)),...  81.3 us
    unnamed x1, local copies, waits for them, and re-layouts  3.09 us

commit v1 on v0

v1 whole, which is shorter than its diff:
```python
import functools
import math

import jax
import jax.numpy as jnp
import numpy as np
from jax import lax
from jax.experimental import pallas as pl
from jax.experimental.pallas import tpu as pltpu
from jax.sharding import PartitionSpec as P

MESH = pl.DeviceIdType.MESH
f32, bf16 = jnp.float32, jnp.bfloat16


def signed(count):
    j = np.arange(count)
    return np.where(j < count // 2, j, j - count)


def high_low(table):
    high = table.astype(np.float32).astype(bf16)
    low = (table - high.astype(np.float64)).astype(np.float32).astype(bf16)
    return high, low


def tables(n, keep, devices):
    k = signed(keep)
    phase = 2.0 * math.pi / n * np.mod(k[:, None] * np.arange(n)[None, :], n)
    cos, sin = np.cos(phase) / math.sqrt(n), np.sin(phase) / math.sqrt(n)
    half = keep // 2
    tx = []
    for b in range(2):
        rows = slice(b * half, (b + 1) * half)
        high, low = high_low(np.concatenate([cos[rows].T, -sin[rows].T], axis=1))
        tx.append(np.concatenate([high, low, high], axis=0))
    ty = []
    for p in range(2):
        high, low = high_low(np.concatenate([cos[p::2, : n // 2], sin[p::2, : n // 2]], axis=0))
        ty.append(np.concatenate([high, low, high], axis=1))
    order = np.arange(n).reshape(devices, n // devices).T.reshape(-1)
    high, low = high_low(np.concatenate([cos[:, order], sin[:, order]], axis=0))
    tz = np.concatenate([high, low, high], axis=1)
    return np.stack(tx), np.stack(ty), tz


def split(x):
    high = x.astype(bf16)
    return high, (x - high.astype(f32)).astype(bf16)


def kernel(
    dims, v_hbm, w_hbm, tx_hbm, ty_hbm, tz_hbm, out,
    v, w, tx, ty, tz, own, away, arrived, outbox, inbox, spec,
    in_sem, t_sem, xs_sem, xr_sem, self_sem, s_sem, r_sem, plane_sem, all_sem,
):
    ny, nz, nx, planes, keep, n = dims
    half = keep // 2
    group = ny * nz * nx
    quad = 4 * planes
    me = lax.axis_index("section") * (group // 2) + lax.axis_index("pen")
    slab = lax.axis_index("slab")
    mx, mz, my = me & (nx - 1), (me // nx) & (nz - 1), me // (nx * nz)

    def device(t, s):
        return {"section": t // (group // 2), "pen": t & (group // 2 - 1), "slab": s}

    far_first = [nz // 2 + ((j + 1) // 2) * (2 * (j % 2) - 1) for j in range(nz)]

    def each_peer(body, steps=far_first):
        for dz in steps:
            line = ((mz + dz) & (nz - 1)) * nx

            def step(i, carry, line=line):
                ty = (my + i // nx) & (ny - 1)
                tx = (mx + i) & (nx - 1)
                body(ty * (nx * nz) + line + tx)
                return carry

            lax.fori_loop(1 if dz % nz == 0 else 0, nx * ny, step, 0)

    loads = [
        pltpu.make_async_copy(tx_hbm, tx, t_sem.at[0]),
        pltpu.make_async_copy(ty_hbm, ty, t_sem.at[1]),
        pltpu.make_async_copy(tz_hbm, tz, t_sem.at[2]),
    ]
    inputs = {}
    for c in (1, 2, 0):
        for i, (src, dst) in enumerate(((v_hbm, v), (w_hbm, w))):
            inputs[c, i] = pltpu.make_async_copy(src.at[c], dst.at[c], in_sem.at[2 * c + i])
            inputs[c, i].start()
        if c == 2:
            loads[0].start()
    loads[1].start()
    loads[2].start()

    barrier = pltpu.get_barrier_semaphore()

    def greet(t, semaphore, s=slab):
        pl.semaphore_signal(semaphore, inc=1, device_id=device(t, s), device_id_type=MESH)

    def across_z():
        return [my * (nx * nz) + ((mz + d) & (nz - 1)) * nx + mx for d in far_first if d % nz]

    def across_x():
        return [me - mx + ((mx + d) & (nx - 1)) for d in (2, 1, 3)]

    def across_y():
        return [((my + d) & (ny - 1)) * (nx * nz) + mz * nx + mx for d in (2, 1, 3)]

    with jax.named_scope("greet"):
        lines = across_z() + across_x() + across_y()
        for t in lines:
            greet(t, barrier)
        greet(me, barrier, 1 - slab)

    def swap(p):
        return pltpu.make_async_remote_copy(
            src_ref=away.at[p],
            dst_ref=arrived.at[p],
            send_sem=xs_sem.at[p],
            recv_sem=xr_sem.at[p],
            device_id=device(me, 1 - slab),
            device_id_type=MESH,
        )

    def x_component(c):
        a, b = (c + 1) % 3, (c + 2) % 3

        def x_plane(z, carry):
            p = v[a, z] * w[b, z] - v[b, z] * w[a, z]
            high, low = split(p)
            lhs = jnp.concatenate([high, high, low], axis=1)
            away[c * planes + z] = jnp.dot(lhs, tx[1 - slab], preferred_element_type=f32)
            own[c * planes + z] = jnp.dot(lhs, tx[slab], preferred_element_type=f32)
            return carry

        with jax.named_scope("x"):
            lax.fori_loop(0, planes, x_plane, 0)

    sign = (1 - 2 * slab).astype(f32)

    def y_component(c):
        def y_plane(z, carry):
            p = c * planes + z
            swap(p).wait_recv()
            mine, other = own[p], arrived[p]
            for parity, folded in enumerate((mine + other, sign * (mine - other))):
                high, low = split(folded)
                both = jnp.dot(
                    ty[parity],
                    jnp.concatenate([high, high, low], axis=0),
                    preferred_element_type=f32,
                )
                row = z * 4 + parity * 2
                outbox[c, pl.ds(row, half, stride=quad), :] = both[:half, :half] + both[half:, half:]
                outbox[c, pl.ds(row + 1, half, stride=quad), :] = (
                    both[:half, half:] - both[half:, :half]
                )
            return carry

        with jax.named_scope("y"):
            lax.fori_loop(0, planes, y_plane, 0)

    def send_component(c):
        def send(t):
            pltpu.make_async_remote_copy(
                src_ref=outbox.at[c, pl.ds(t * quad, quad)],
                dst_ref=inbox.at[c, pl.ds(me * quad, quad)],
                send_sem=s_sem.at[c],
                recv_sem=r_sem.at[c],
                device_id=device(t, slab),
                device_id_type=MESH,
            ).start()

        with jax.named_scope("send"):
            each_peer(send)
        pltpu.make_async_copy(
            outbox.at[c, pl.ds(me * quad, quad)], inbox.at[c, pl.ds(me * quad, quad)], self_sem.at[c]
        ).start()

    def swap_component(c):
        for z in range(planes):
            swap(c * planes + z).start()

    for key in ((1, 0), (1, 1), (2, 0), (2, 1)):
        inputs[key].wait()
    loads[0].wait()
    x_component(0)
    with jax.named_scope("lines"):
        pl.semaphore_wait(barrier, len(lines) + 1)
    swap_component(0)
    for t in across_x():
        greet(t, plane_sem)
    for key in ((0, 0), (0, 1)):
        inputs[key].wait()
    x_component(1)
    swap_component(1)
    with jax.named_scope("plane"):
        pl.semaphore_wait(plane_sem, nx - 1)
    for t in across_y():
        greet(t, all_sem)
    loads[1].wait()
    y_component(0)
    with jax.named_scope("all"):
        pl.semaphore_wait(all_sem, ny - 1)
    send_component(0)
    x_component(2)
    swap_component(2)
    y_component(1)
    send_component(1)
    y_component(2)
    send_component(2)
    loads[2].wait()

    def z_component(c, carry):
        some = pl.ds(0, (group - 1) * quad)
        with jax.named_scope("recv"):
            pltpu.make_async_copy(outbox.at[c, some], inbox.at[c, some], r_sem.at[c]).wait()
        pltpu.make_async_copy(
            outbox.at[c, pl.ds(me * quad, quad)], inbox.at[c, pl.ds(me * quad, quad)], self_sem.at[c]
        ).wait()
        with jax.named_scope("z"):
            for q in range(2):
                pieces = [
                    jnp.concatenate(
                        [inbox[c, pl.ds(r * 4 + q * 2 + part, group, stride=quad), :] for r in range(planes)],
                        axis=0,
                    )
                    for part in range(2)
                ]
                high, low = split(jnp.concatenate(pieces, axis=1))
                both = jnp.dot(
                    tz[...], jnp.concatenate([high, high, low], axis=0), preferred_element_type=f32
                )
                spec[c, 2 * q] = both[:keep, :half] + both[keep:, half:]
                spec[c, 2 * q + 1] = both[:keep, half:] - both[keep:, :half]
        return carry

    lax.fori_loop(0, 3, z_component, 0)

    limit = -half
    to_wave = lambda j: jnp.where(j < half, j, j - keep)
    kz = to_wave(lax.broadcasted_iota(jnp.int32, (keep, half), 0))
    kx = to_wave(slab * half + lax.broadcasted_iota(jnp.int32, (keep, half), 1))
    with jax.named_scope("project"):
        for q in range(2):
            ky = jnp.full((keep, half), to_wave(2 * me + q), jnp.int32)
            kept = ((kx != limit) & (ky != limit) & (kz != limit)).astype(f32)
            waves = (kx.astype(f32), ky.astype(f32), kz.astype(f32))
            ksq = waves[0] * waves[0] + waves[1] * waves[1] + waves[2] * waves[2]
            scale = 1.0 / jnp.maximum(ksq, 1.0)
            for part in range(2):
                row = 2 * q + part
                s = [spec[c, row] for c in range(3)]
                inner = (waves[0] * s[0] + waves[1] * s[1] + waves[2] * s[2]) * scale
                for c in range(3):
                    rows = pl.ds(row, keep, stride=4)
                    out[c, rows, :] = (s[c] - waves[c] * inner) * kept
    with jax.named_scope("drain"):
        for p in range(3 * planes):
            swap(p).wait_send()
        for c in range(3):
            some = pl.ds(0, (group - 1) * quad)
            pltpu.make_async_copy(outbox.at[c, some], inbox.at[c, some], s_sem.at[c]).wait()


def per_device(sizes, velocity, vorticity, velocity_modes):
    ny, nz, nx = sizes
    _, planes, rows, n = velocity.shape
    keep, half = velocity_modes.shape[1], velocity_modes.shape[4]
    group = ny * nz * nx
    tx, ty, tz = tables(n, keep, group)
    anywhere = pl.BlockSpec(memory_space=pltpu.HBM)
    quad = 4 * planes
    dma = pltpu.SemaphoreType.DMA
    out = pl.pallas_call(
        functools.partial(kernel, (ny, nz, nx, planes, keep, n)),
        out_shape=jax.ShapeDtypeStruct((3, 4 * keep, half), f32),
        in_specs=[anywhere] * 5,
        out_specs=pl.BlockSpec(memory_space=pltpu.VMEM),
        scratch_shapes=[
            pltpu.VMEM((3, planes, rows, n), f32),
            pltpu.VMEM((3, planes, rows, n), f32),
            pltpu.VMEM(tx.shape, bf16),
            pltpu.VMEM(ty.shape, bf16),
            pltpu.VMEM(tz.shape, bf16),
            pltpu.VMEM((3 * planes, rows, keep), f32),
            pltpu.VMEM((3 * planes, rows, keep), f32),
            pltpu.VMEM((3 * planes, rows, keep), f32),
            pltpu.VMEM((3, group * quad, half), f32),
            pltpu.VMEM((3, group * quad, half), f32),
            pltpu.VMEM((3, 4, keep, half), f32),
            dma((6,)),
            dma((3,)),
            dma((3 * planes,)),
            dma((3 * planes,)),
            dma((3,)),
            dma((3,)),
            dma((3,)),
            pltpu.SemaphoreType.REGULAR,
            pltpu.SemaphoreType.REGULAR,
        ],
        compiler_params=pltpu.CompilerParams(
            collective_id=0, has_side_effects=True, vmem_limit_bytes=28 << 20
        ),
    )(*(pltpu.with_memory_space_constraint(x, pltpu.HBM) for x in (velocity, vorticity, tx, ty, tz)))
    shape = (4 * keep, half)
    row = lax.broadcasted_iota(jnp.int32, shape, 0)
    me = lax.axis_index("section") * (group // 2) + lax.axis_index("pen")
    to_wave = lambda j: jnp.where(j < half, j, j - keep).astype(f32)
    kz, ky = to_wave(row // 4), to_wave(2 * me + (row // 2) % 2)
    kx = to_wave(lax.axis_index("slab") * half + lax.broadcasted_iota(jnp.int32, shape, 1))
    viscous = 0.5 / half**2 * (kx * kx + ky * ky + kz * kz)
    rhs = out - viscous * velocity_modes.reshape(3, *shape)
    return rhs.reshape(velocity_modes.shape)


def solution(mesh):
    sizes = (4, 8, 4)
    return jax.shard_map(
        functools.partial(per_device, sizes),
        mesh=mesh,
        in_specs=(
            P(None, ("section", "pen"), "slab", None),
            P(None, ("section", "pen"), "slab", None),
            P(None, None, ("section", "pen"), None, "slab"),
        ),
        out_specs=P(None, None, ("section", "pen"), None, "slab"),
        check_vma=False,
    )
```

time: 84.5 us -> 73.6 us (0.87)
  Pallas kernels: 81.3 us -> 71.2 us
  local copies, waits for them, and re-layouts: 3.09 us -> 0.01 us
  other arithmetic: 0 us -> 2.23 us
    pallas_call x1, Pallas kernels: 81.3 us -> 71.2 us  [per_device(): pl.pallas_call(functools.partial(kernel, (ny, nz, nx, planes, keep, n)),...]
    unnamed x1 -> x2, local copies, waits for them, and re-layouts: 3.09 us -> 0.01 us
    sub x0 -> x2, other arithmetic: none -> 1.32 us  [the longest x1 1.32 us: per_device(): rhs = out - viscous * velocity_modes.reshape(3, *shape)]
    mul x0 -> x1, other arithmetic: none -> 0.88 us  [per_device(): viscous = 0.5 / half ** 2 * (kx * kx + ky * ky + kz * kz)]
where the time goes in v1:
time: 73.6 us; the launch traced here: 73.5 us
  Pallas kernels  71.2 us (97%)
  other arithmetic  2.23 us (3%)
    pallas_call x1, Pallas kernels, per_device(): pl.pallas_call(functools.partial(kernel, (ny, nz, nx, planes, keep, n)),...  71.2 us

profile of v1, /device:TPU:1, one launch (start us, length us, event | category | flops | bytes accessed | tf_op | source)
XLA Modules:
  0.0 73.5 jit_solution(15859603166437270011)
XLA Ops:
  0.1 0.9 %fusion.6 = f32[1024,128]{1,0:T(8,128)S(1)} fusion(s32[1024]{0:T(1024)S(1)} %get-tuple-element.8, s32[1024]{0:T(1024)S(1)} %get-tuple-element.11, s32[1024]{0:T(1024)S(1)} %get-tuple-element.7, s32[1024]{0:T(1024)S(1)} %get-tuple-element.12, s32[]{:T(128)S(6)} %mul.51, s32[128]{0:T(128)S(1)} %get-tuple-element.6, s32[128]{0:T(128)S(1)} %get-tuple-element.5, ...), kind=kLoop, calls=%fused_computation.14 | loop fusion | flops 3932160 | bytes 543876 | tf_op jit(solution)/shard_map/mul | solution.py:314
  0.9 0.0 copy-start
  1.0 71.2 %shard_map.64 = f32[3,1024,128]{2,1,0:T(8,128)S(1)} custom-call(f32[3,3,192,384]{3,2,1,0:T(8,128)} %v_hbm.1, f32[3,3,192,384]{3,2,1,0:T(8,128)} %w_hbm.1, bf16[2,1152,256]{2,1,0:T(8,128)(2,1)} %constant.72.clone.tx_hbm, bf16[2,256,576]{2,1,0:T(8,128)(2,1)} %constant.73.clone.ty_hbm, bf16[512,1152]{1,0:T(8,128)(2,1)} %constant.74.clone.tz_hbm), custom_call_target="tpu_custom_call" | custom-call | tf_op jit(solution)/shard_map/pallas_call | solution.py:277
  72.2 0.0 copy-done
  72.2 1.3 %multiply_subtract_fusion = f32[3,1024,128]{2,1,0:T(8,128)} fusion(f32[3,1024,128]{2,1,0:T(8,128)S(1)} %shard_map.64, f32[3,1024,128]{2,1,0:T(8,128)S(1)} %bitcast.2, f32[1024,128]{1,0:T(8,128)S(1)} %fusion.6), kind=kLoop, calls=%fused_computation | loop fusion | flops 786432 | bytes 5242880 | tf_op jit(solution)/shard_map/sub | solution.py:315
  (5 shorter events, 0.0 us)
Async XLA Ops:
  0.9 71.3 %copy-start = (f32[3,256,2,2,128]{4,3,2,1,0:T(2,128)S(1)}, f32[3,256,2,2,128]{4,3,2,1,0:T(2,128)}, u32[]{:S(2)}) copy-start(f32[3,256,2,2,128]{4,3,2,1,0:T(2,128)} %param.8) | copy-start | bytes 4718596

commit v2 on v1

v2 whole, which is shorter than its diff:
```python
import functools
import math

import jax
import jax.numpy as jnp
import numpy as np
from jax import lax
from jax.experimental import pallas as pl
from jax.experimental.pallas import tpu as pltpu
from jax.sharding import PartitionSpec as P

MESH = pl.DeviceIdType.MESH
f32, bf16 = jnp.float32, jnp.bfloat16


def signed(count):
    j = np.arange(count)
    return np.where(j < count // 2, j, j - count)


def high_low(table):
    high = table.astype(np.float32).astype(bf16)
    low = (table - high.astype(np.float64)).astype(np.float32).astype(bf16)
    return high, low


def tables(n, keep, devices):
    k = signed(keep)
    phase = 2.0 * math.pi / n * np.mod(k[:, None] * np.arange(n)[None, :], n)
    cos, sin = np.cos(phase) / math.sqrt(n), np.sin(phase) / math.sqrt(n)
    half = keep // 2
    tx = []
    for b in range(2):
        rows = slice(b * half, (b + 1) * half)
        high, low = high_low(np.concatenate([cos[rows].T, -sin[rows].T], axis=1))
        tx.append(np.concatenate([high, low, high], axis=0))
    ty = []
    for p in range(2):
        high, low = high_low(np.concatenate([cos[p::2, : n // 2], sin[p::2, : n // 2]], axis=0))
        ty.append(np.concatenate([high, low, high], axis=1))
    order = np.arange(n).reshape(devices, n // devices).T.reshape(-1)
    high, low = high_low(np.concatenate([cos[:, order], sin[:, order]], axis=0))
    tz = np.concatenate([high, low, high], axis=1)
    return np.stack(tx), np.stack(ty), tz


def split(x):
    high = x.astype(bf16)
    return high, (x - high.astype(f32)).astype(bf16)


def kernel(
    dims, v_hbm, w_hbm, m_hbm, tx_hbm, ty_hbm, tz_hbm, out, viscous,
    v, w, modes, tx, ty, tz, own, away, arrived, outbox, inbox, spec,
    in_sem, m_sem, t_sem, xs_sem, xr_sem, self_sem, s_sem, r_sem, plane_sem, all_sem,
):
    ny, nz, nx, planes, keep, n = dims
    half = keep // 2
    group = ny * nz * nx
    quad = 4 * planes
    me = lax.axis_index("section") * (group // 2) + lax.axis_index("pen")
    slab = lax.axis_index("slab")
    mx, mz, my = me & (nx - 1), (me // nx) & (nz - 1), me // (nx * nz)

    def device(t, s):
        return {"section": t // (group // 2), "pen": t & (group // 2 - 1), "slab": s}

    far_first = [nz // 2 + ((j + 1) // 2) * (2 * (j % 2) - 1) for j in range(nz)]

    def far(j, count):
        return count // 2 + ((j + 1) // 2) * (2 * (j & 1) - 1)

    def each_peer(body, first=0, last=nx * ny):
        def step(i, carry):
            ty = (my + far(i // nx, ny)) & (ny - 1)
            tx = (mx + far(i & (nx - 1), nx)) & (nx - 1)
            for dz in far_first:
                body(ty * (nx * nz) + ((mz + dz) & (nz - 1)) * nx + tx)
            return carry

        lax.fori_loop(first, min(last, nx * ny - 1), step, 0)
        if last == nx * ny:
            for dz in far_first:
                if dz % nz:
                    body(me - mz * nx + ((mz + dz) & (nz - 1)) * nx)

    x_table = pltpu.make_async_copy(tx_hbm, tx, t_sem.at[0])
    y_table = pltpu.make_async_copy(ty_hbm, ty, t_sem.at[1])
    z_table = pltpu.make_async_copy(tz_hbm, tz, t_sem.at[2])
    mode_load = pltpu.make_async_copy(m_hbm, modes, m_sem)
    fields = [
        [
            pltpu.make_async_copy(src.at[c, z], dst.at[c, z], in_sem.at[4 * z + i])
            for i, (src, dst, c) in enumerate(
                ((v_hbm, v, 1), (w_hbm, w, 2), (v_hbm, v, 2), (w_hbm, w, 1))
            )
        ]
        for z in range(planes)
    ] + [
        [
            pltpu.make_async_copy(src.at[0], dst.at[0], in_sem.at[4 * planes + i])
            for i, (src, dst) in enumerate(((v_hbm, v), (w_hbm, w)))
        ]
    ]

    def start(*copies):
        for copy in copies:
            copy.start()

    start(*fields[0], x_table)

    barrier = pltpu.get_barrier_semaphore()

    def greet(t, semaphore, s=slab):
        pl.semaphore_signal(semaphore, inc=1, device_id=device(t, s), device_id_type=MESH)

    def across_z():
        return [my * (nx * nz) + ((mz + d) & (nz - 1)) * nx + mx for d in far_first if d % nz]

    def across_x():
        return [me - mx + ((mx + d) & (nx - 1)) for d in (2, 1, 3)]

    def across_y():
        return [((my + d) & (ny - 1)) * (nx * nz) + mz * nx + mx for d in (2, 1, 3)]

    with jax.named_scope("greet"):
        lines = across_z() + across_x() + across_y()
        for t in lines:
            greet(t, barrier)
        greet(me, barrier, 1 - slab)
    start(*fields[1])

    def swap(p):
        return pltpu.make_async_remote_copy(
            src_ref=away.at[p],
            dst_ref=arrived.at[p],
            send_sem=xs_sem.at[p],
            recv_sem=xr_sem.at[p],
            device_id=device(me, 1 - slab),
            device_id_type=MESH,
        )

    def x_plane(c, z):
        a, b = (c + 1) % 3, (c + 2) % 3
        p = v[a, z] * w[b, z] - v[b, z] * w[a, z]
        high, low = split(p)
        lhs = jnp.concatenate([high, high, low], axis=1)
        away[c * planes + z] = jnp.dot(lhs, tx[1 - slab], preferred_element_type=f32)
        own[c * planes + z] = jnp.dot(lhs, tx[slab], preferred_element_type=f32)

    sign = (1 - 2 * slab).astype(f32)

    def row_of(c, z, q, part):
        return q * 2 * planes + z * 2 + part if c == 2 else z * 4 + q * 2 + part

    def y_plane(c, z):
        p = c * planes + z
        swap(p).wait_recv()
        mine, other = own[p], arrived[p]
        for q, folded in enumerate((mine + other, sign * (mine - other))):
            high, low = split(folded)
            both = jnp.dot(
                ty[q],
                jnp.concatenate([high, high, low], axis=0),
                preferred_element_type=f32,
            )
            outbox[c, pl.ds(row_of(c, z, q, 0), half, stride=quad), :] = (
                both[:half, :half] + both[half:, half:]
            )
            outbox[c, pl.ds(row_of(c, z, q, 1), half, stride=quad), :] = (
                both[:half, half:] - both[half:, :half]
            )

    def send(c, part, row, rows, **which):
        def one(t):
            pltpu.make_async_remote_copy(
                src_ref=outbox.at[c, pl.ds(t * quad + row, rows)],
                dst_ref=inbox.at[c, pl.ds(me * quad + row, rows)],
                send_sem=s_sem.at[part],
                recv_sem=r_sem.at[part],
                device_id=device(t, slab),
                device_id_type=MESH,
            ).start()

        with jax.named_scope("send"):
            each_peer(one, **which)

    def keep_own(c):
        return pltpu.make_async_copy(
            outbox.at[c, pl.ds(me * quad, quad)], inbox.at[c, pl.ds(me * quad, quad)], self_sem.at[c]
        )

    def looped(body, c):
        def step(z, carry):
            body(c, z)
            return carry

        lax.fori_loop(0, planes, step, 0)

    with jax.named_scope("x0"):
        for z in range(planes):
            for copy in fields[z]:
                copy.wait()
            if z == 0:
                x_table.wait()
                start(*fields[2], y_table, *fields[3])
            x_plane(0, z)
            if z == 0:
                with jax.named_scope("lines"):
                    pl.semaphore_wait(barrier, len(lines) + 1)
                for t in across_x():
                    greet(t, plane_sem)
            swap(z).start()
    start(z_table, mode_load)
    for copy in fields[planes]:
        copy.wait()
    x_plane(1, 0)
    with jax.named_scope("plane"):
        pl.semaphore_wait(plane_sem, nx - 1)
    for t in across_y():
        greet(t, all_sem)
    y_table.wait()
    for z in range(planes):
        with jax.named_scope("y0"):
            y_plane(0, z)
        send(0, 0, z * 4, 4, first=nx * (ny - 1))
    with jax.named_scope("all"):
        pl.semaphore_wait(all_sem, ny - 1)
    send(0, 0, 0, quad, last=nx * (ny - 1))
    keep_own(0).start()
    swap(planes).start()
    for z in range(1, planes):
        x_plane(1, z)
        swap(planes + z).start()
    with jax.named_scope("y1"):
        looped(y_plane, 1)
    send(1, 1, 0, quad)
    keep_own(1).start()
    with jax.named_scope("x2"):
        looped(x_plane, 2)
    for z in range(planes):
        swap(2 * planes + z).start()
    with jax.named_scope("y2"):
        looped(y_plane, 2)
    for q in range(2):
        send(2, 2 + q, q * 2 * planes, 2 * planes)
    keep_own(2).start()

    limit = -half
    visc = 0.5 / half**2
    to_wave = lambda j: jnp.where(j < half, j, j - keep)
    kz = to_wave(lax.broadcasted_iota(jnp.int32, (keep, half), 0))
    kx = to_wave(slab * half + lax.broadcasted_iota(jnp.int32, (keep, half), 1))

    def waves_of(q):
        ky = jnp.full((keep, half), to_wave(2 * me + q), jnp.int32)
        kept = ((kx != limit) & (ky != limit) & (kz != limit)).astype(f32)
        waves = (kx.astype(f32), ky.astype(f32), kz.astype(f32))
        ksq = waves[0] * waves[0] + waves[1] * waves[1] + waves[2] * waves[2]
        return waves, ksq, kept

    mode_load.wait()
    with jax.named_scope("viscous"):
        for q in range(2):
            _, ksq, _ = waves_of(q)
            for part in range(2):
                rows = pl.ds(2 * q + part, keep, stride=4)
                for c in range(3):
                    viscous[c, rows, :] = visc * ksq * modes[c, rows, :]
    z_table.wait()

    def z_rows(c, q):
        pieces = [
            jnp.concatenate(
                [inbox[c, pl.ds(row_of(c, r, q, part), group, stride=quad), :] for r in range(planes)],
                axis=0,
            )
            for part in range(2)
        ]
        high, low = split(jnp.concatenate(pieces, axis=1))
        parts = jnp.concatenate([high, high, low], axis=0)
        cos = jnp.dot(tz[:keep], parts, preferred_element_type=f32)
        sin = jnp.dot(tz[keep:], parts, preferred_element_type=f32)
        spec[c, 2 * q] = cos[:, :half] + sin[:, half:]
        spec[c, 2 * q + 1] = cos[:, half:] - sin[:, :half]

    def project(q):
        waves, ksq, kept = waves_of(q)
        scale = 1.0 / jnp.maximum(ksq, 1.0)
        for part in range(2):
            row = 2 * q + part
            s = [spec[c, row] for c in range(3)]
            inner = (waves[0] * s[0] + waves[1] * s[1] + waves[2] * s[2]) * scale
            for c in range(3):
                out[c, pl.ds(row, keep, stride=4), :] = (s[c] - waves[c] * inner) * kept

    def arrived_bytes(c, part, rows, sem):
        some = pl.ds(0, (group - 1) * rows)
        pltpu.make_async_copy(outbox.at[c, some], inbox.at[c, some], sem.at[part]).wait()

    for c in range(2):
        with jax.named_scope("recv"):
            arrived_bytes(c, c, quad, r_sem)
        keep_own(c).wait()
        with jax.named_scope("z"):
            for q in range(2):
                z_rows(c, q)
    keep_own(2).wait()
    for q in range(2):
        with jax.named_scope("recv"):
            arrived_bytes(2, 2 + q, 2 * planes, r_sem)
        with jax.named_scope("z"):
            z_rows(2, q)
        with jax.named_scope("project"):
            project(q)

    with jax.named_scope("drain"):
        for p in range(3 * planes):
            swap(p).wait_send()
        for part, (c, rows) in enumerate(((0, quad), (1, quad), (2, 2 * planes), (2, 2 * planes))):
            arrived_bytes(c, part, rows, s_sem)


def per_device(sizes, velocity, vorticity, velocity_modes):
    ny, nz, nx = sizes
    _, planes, rows, n = velocity.shape
    keep, half = velocity_modes.shape[1], velocity_modes.shape[4]
    group = ny * nz * nx
    tx, ty, tz = tables(n, keep, group)
    quad = 4 * planes
    dma = pltpu.SemaphoreType.DMA
    whole = jax.ShapeDtypeStruct((3, 4 * keep, half), f32)
    operands = (velocity, vorticity, velocity_modes.reshape(whole.shape), tx, ty, tz)
    projected, viscous = pl.pallas_call(
        functools.partial(kernel, (ny, nz, nx, planes, keep, n)),
        out_shape=(whole, whole),
        in_specs=[pl.BlockSpec(memory_space=pltpu.HBM)] * 6,
        out_specs=(pl.BlockSpec(memory_space=pltpu.VMEM),) * 2,
        scratch_shapes=[
            pltpu.VMEM((3, planes, rows, n), f32),
            pltpu.VMEM((3, planes, rows, n), f32),
            pltpu.VMEM(whole.shape, f32),
            pltpu.VMEM(tx.shape, bf16),
            pltpu.VMEM(ty.shape, bf16),
            pltpu.VMEM(tz.shape, bf16),
            pltpu.VMEM((3 * planes, rows, keep), f32),
            pltpu.VMEM((3 * planes, rows, keep), f32),
            pltpu.VMEM((3 * planes, rows, keep), f32),
            pltpu.VMEM((3, group * quad, half), f32),
            pltpu.VMEM((3, group * quad, half), f32),
            pltpu.VMEM((3, 4, keep, half), f32),
            dma((4 * planes + 2,)),
            dma,
            dma((3,)),
            dma((3 * planes,)),
            dma((3 * planes,)),
            dma((3,)),
            dma((4,)),
            dma((4,)),
            pltpu.SemaphoreType.REGULAR,
            pltpu.SemaphoreType.REGULAR,
        ],
        compiler_params=pltpu.CompilerParams(
            collective_id=0, has_side_effects=True, vmem_limit_bytes=30 << 20
        ),
    )(*(pltpu.with_memory_space_constraint(x, pltpu.HBM) for x in operands))
    return (projected - viscous).reshape(velocity_modes.shape)


def solution(mesh):
    sizes = (4, 8, 4)
    return jax.shard_map(
        functools.partial(per_device, sizes),
        mesh=mesh,
        in_specs=(
            P(None, ("section", "pen"), "slab", None),
            P(None, ("section", "pen"), "slab", None),
            P(None, None, ("section", "pen"), None, "slab"),
        ),
        out_specs=P(None, None, ("section", "pen"), None, "slab"),
        check_vma=False,
    )
```

time: 73.6 us -> 67.7 us (0.920)
  Pallas kernels: 71.2 us -> 66.3 us
  other arithmetic: 2.23 us -> 1.3 us
    pallas_call x1, Pallas kernels: 71.2 us -> 66.3 us  [per_device(): pl.pallas_call(functools.partial(kernel, (ny, nz, nx, planes, keep, n)),...]
    mul x1 -> x0, other arithmetic: 0.88 us -> none  [per_device(): viscous = 0.5 / half ** 2 * (kx * kx + ky * ky + kz * kz)]
where the time goes in v2:
time: 67.7 us; the launch traced here: 67.6 us
  Pallas kernels  66.3 us (98%)
  other arithmetic  1.3 us (2%)
    pallas_call x1, Pallas kernels, per_device(): pl.pallas_call(functools.partial(kernel, (ny, nz, nx, planes, keep, n)),...  66.3 us

profile of v2, /device:TPU:1, one launch (start us, length us, event | category | flops | bytes accessed | tf_op | source)
XLA Modules:
  0.0 67.6 jit_solution(1025501313819765146)
XLA Ops:
  0.0 66.3 %shard_map.64 = (f32[3,1024,128]{2,1,0:T(8,128)S(1)}, f32[3,1024,128]{2,1,0:T(8,128)S(1)}) custom-call(f32[3,3,192,384]{3,2,1,0:T(8,128)} %v_hbm.1, f32[3,3,192,384]{3,2,1,0:T(8,128)} %w_hbm.1, f32[3,1024,128]{2,1,0:T(8,128)} %bitcast.2, bf16[2,1152,256]{2,1,0:T(8,128)(2,1)} %constant.6.clone.tx_hbm, bf16[2,256,576]{2,1,0:T(8,128)(2,1)} %constant.7.clone.ty_hbm, ...), custom_call_target="tpu_custom_call" | custom-call | tf_op jit(solution)/shard_map/pallas_call | solution.py:334
  66.3 1.3 %sub.3 = f32[3,1024,128]{2,1,0:T(8,128)} subtract(f32[3,1024,128]{2,1,0:T(8,128)S(1)} %get-tuple-element.7, f32[3,1024,128]{2,1,0:T(8,128)S(1)} %get-tuple-element.8) | non-fusion elementwise | flops 393216 | bytes 4718592 | tf_op jit(solution)/shard_map/sub | solution.py:367

commit v3 on v2

--- a/solution.py
+++ b/solution.py
@@ -11,6 +11,10 @@
 
 MESH = pl.DeviceIdType.MESH
 f32, bf16 = jnp.float32, jnp.bfloat16
+
+
+PLACES = (0, 1, 4, 5, 2, 3, 6, 7)
+EARLY = 4
 
 
 def signed(count):
@@ -70,19 +74,54 @@
     def far(j, count):
         return count // 2 + ((j + 1) // 2) * (2 * (j & 1) - 1)
 
-    def each_peer(body, first=0, last=nx * ny):
+    def each_peer(body, first=0, last=nx * ny, near=False):
+        turn = far_first[::-1] if near else far_first
+
         def step(i, carry):
+            if near:
+                i = nx * ny - 1 - i
             ty = (my + far(i // nx, ny)) & (ny - 1)
             tx = (mx + far(i & (nx - 1), nx)) & (nx - 1)
-            for dz in far_first:
+            for dz in turn:
                 body(ty * (nx * nz) + ((mz + dz) & (nz - 1)) * nx + tx)
             return carry
 
-        lax.fori_loop(first, min(last, nx * ny - 1), step, 0)
-        if last == nx * ny:
-            for dz in far_first:
+        def own_line():
+            for dz in turn:
                 if dz % nz:
                     body(me - mz * nx + ((mz + dz) & (nz - 1)) * nx)
+
+        if near:
+            if last == nx * ny:
+                own_line()
+            lax.fori_loop(max(nx * ny - last, 1), nx * ny - first, step, 0)
+        else:
+            lax.fori_loop(first, min(last, nx * ny - 1), step, 0)
+            if last == nx * ny:
+                own_line()
+
+    def each_peer_by_place(body):
+        def step(i, carry, corner):
+            ty = (my + far(i // nx, ny)) & (ny - 1)
+            tx = (mx + far(i & (nx - 1), nx)) & (nx - 1)
+            for z in range(EARLY) if corner else PLACES:
+                t = (ty * nz + z) * nx + tx
+                if corner or z < EARLY:
+                    wanted = ((tx == 0) | (ty == 0)) == corner
+
+                    @pl.when(wanted & (me != t))
+                    def _(t=t):
+                        body(t)
+                else:
+
+                    @pl.when(me != t)
+                    def _(t=t):
+                        body(t)
+
+            return carry
+
+        for corner in (True, False):
+            lax.fori_loop(0, nx * ny, functools.partial(step, corner=corner), 0)
 
     x_table = pltpu.make_async_copy(tx_hbm, tx, t_sem.at[0])
     y_table = pltpu.make_async_copy(ty_hbm, ty, t_sem.at[1])
@@ -150,8 +189,17 @@
 
     sign = (1 - 2 * slab).astype(f32)
 
+    widths = (quad, quad + 2 * planes, 2 * planes)
+    bases = (0, group * widths[0], group * (widths[0] + widths[1]))
+
     def row_of(c, z, q, part):
-        return q * 2 * planes + z * 2 + part if c == 2 else z * 4 + q * 2 + part
+        if c < 2:
+            return bases[c], widths[c], z * 4 + q * 2 + part
+        return bases[1 + q], widths[1 + q], (1 - q) * quad + z * 2 + part
+
+    def rows_of(c, z, q, part):
+        base, width, row = row_of(c, z, q, part)
+        return pl.ds(base + row, group, stride=width)
 
     def y_plane(c, z):
         p = c * planes + z
@@ -164,18 +212,23 @@
                 jnp.concatenate([high, high, low], axis=0),
                 preferred_element_type=f32,
             )
-            outbox[c, pl.ds(row_of(c, z, q, 0), half, stride=quad), :] = (
+            outbox[rows_of(c, z, q, 0), :] = (
                 both[:half, :half] + both[half:, half:]
             )
-            outbox[c, pl.ds(row_of(c, z, q, 1), half, stride=quad), :] = (
+            outbox[rows_of(c, z, q, 1), :] = (
                 both[:half, half:] - both[half:, :half]
             )
 
-    def send(c, part, row, rows, **which):
+    def message(part, t, row, rows):
+        return pl.ds(bases[part] + t * widths[part] + row, rows)
+
+    def send(part, row=0, rows=None, by_place=False, **which):
+        rows = rows or widths[part]
+
         def one(t):
             pltpu.make_async_remote_copy(
-                src_ref=outbox.at[c, pl.ds(t * quad + row, rows)],
-                dst_ref=inbox.at[c, pl.ds(me * quad + row, rows)],
+                src_ref=outbox.at[message(part, t, row, rows)],
+                dst_ref=inbox.at[message(part, me, row, rows)],
                 send_sem=s_sem.at[part],
                 recv_sem=r_sem.at[part],
                 device_id=device(t, slab),
@@ -183,12 +236,15 @@
             ).start()
 
         with jax.named_scope("send"):
-            each_peer(one, **which)
-
-    def keep_own(c):
-        return pltpu.make_async_copy(
-            outbox.at[c, pl.ds(me * quad, quad)], inbox.at[c, pl.ds(me * quad, quad)], self_sem.at[c]
-        )
+            (each_peer_by_place if by_place else each_peer)(one, **which)
+
+    def keep_own(part):
+        mine = message(part, me, 0, widths[part])
+        return pltpu.make_async_copy(outbox.at[mine], inbox.at[mine], self_sem.at[part])
+
+    def all_of(part, sem):
+        some = pl.ds(bases[part], (group - 1) * widths[part])
+        return pltpu.make_async_copy(outbox.at[some], inbox.at[some], sem.at[part])
 
     def looped(body, c):
         def step(z, carry):
@@ -205,45 +261,46 @@
                 x_table.wait()
                 start(*fields[2], y_table, *fields[3])
             x_plane(0, z)
-            if z == 0:
+            if z == 1:
                 with jax.named_scope("lines"):
                     pl.semaphore_wait(barrier, len(lines) + 1)
                 for t in across_x():
                     greet(t, plane_sem)
-            swap(z).start()
+                swap(0).start()
+            if z > 0:
+                swap(z).start()
     start(z_table, mode_load)
-    for copy in fields[planes]:
-        copy.wait()
-    x_plane(1, 0)
+
+    plane = nx * (ny - 1)
+    y_table.wait()
     with jax.named_scope("plane"):
         pl.semaphore_wait(plane_sem, nx - 1)
     for t in across_y():
         greet(t, all_sem)
-    y_table.wait()
     for z in range(planes):
         with jax.named_scope("y0"):
             y_plane(0, z)
-        send(0, 0, z * 4, 4, first=nx * (ny - 1))
+        send(0, z * 4, 4, first=plane, near=True)
     with jax.named_scope("all"):
         pl.semaphore_wait(all_sem, ny - 1)
-    send(0, 0, 0, quad, last=nx * (ny - 1))
+    send(0, last=plane, near=True)
     keep_own(0).start()
-    swap(planes).start()
-    for z in range(1, planes):
+    for copy in fields[planes]:
+        copy.wait()
+    for z in range(planes):
         x_plane(1, z)
         swap(planes + z).start()
     with jax.named_scope("y1"):
         looped(y_plane, 1)
-    send(1, 1, 0, quad)
-    keep_own(1).start()
     with jax.named_scope("x2"):
         looped(x_plane, 2)
     for z in range(planes):
         swap(2 * planes + z).start()
     with jax.named_scope("y2"):
         looped(y_plane, 2)
-    for q in range(2):
-        send(2, 2 + q, q * 2 * planes, 2 * planes)
+    send(1)
+    keep_own(1).start()
+    send(2, by_place=True)
     keep_own(2).start()
 
     limit = -half
@@ -271,10 +328,7 @@
 
     def z_rows(c, q):
         pieces = [
-            jnp.concatenate(
-                [inbox[c, pl.ds(row_of(c, r, q, part), group, stride=quad), :] for r in range(planes)],
-                axis=0,
-            )
+            jnp.concatenate([inbox[rows_of(c, r, q, part), :] for r in range(planes)], axis=0)
             for part in range(2)
         ]
         high, low = split(jnp.concatenate(pieces, axis=1))
@@ -294,31 +348,22 @@
             for c in range(3):
                 out[c, pl.ds(row, keep, stride=4), :] = (s[c] - waves[c] * inner) * kept
 
-    def arrived_bytes(c, part, rows, sem):
-        some = pl.ds(0, (group - 1) * rows)
-        pltpu.make_async_copy(outbox.at[c, some], inbox.at[c, some], sem.at[part]).wait()
-
-    for c in range(2):
+    for part, ready in enumerate((((0, 0), (0, 1)), ((1, 0), (1, 1), (2, 0)), ((2, 1),))):
         with jax.named_scope("recv"):
-            arrived_bytes(c, c, quad, r_sem)
-        keep_own(c).wait()
+            keep_own(part).wait()
+            all_of(part, r_sem).wait()
         with jax.named_scope("z"):
-            for q in range(2):
+            for c, q in ready:
                 z_rows(c, q)
-    keep_own(2).wait()
-    for q in range(2):
-        with jax.named_scope("recv"):
-            arrived_bytes(2, 2 + q, 2 * planes, r_sem)
-        with jax.named_scope("z"):
-            z_rows(2, q)
-        with jax.named_scope("project"):
-            project(q)
+        if part:
+            with jax.named_scope("project"):
+                project(part - 1)
 
     with jax.named_scope("drain"):
         for p in range(3 * planes):
             swap(p).wait_send()
-        for part, (c, rows) in enumerate(((0, quad), (1, quad), (2, 2 * planes), (2, 2 * planes))):
-            arrived_bytes(c, part, rows, s_sem)
+        for part in range(3):
+            all_of(part, s_sem).wait()
 
 
 def per_device(sizes, velocity, vorticity, velocity_modes):
@@ -346,8 +391,8 @@
             pltpu.VMEM((3 * planes, rows, keep), f32),
             pltpu.VMEM((3 * planes, rows, keep), f32),
             pltpu.VMEM((3 * planes, rows, keep), f32),
-            pltpu.VMEM((3, group * quad, half), f32),
-            pltpu.VMEM((3, group * quad, half), f32),
+            pltpu.VMEM((3 * group * quad, half), f32),
+            pltpu.VMEM((3 * group * quad, half), f32),
             pltpu.VMEM((3, 4, keep, half), f32),
             dma((4 * planes + 2,)),
             dma,
@@ -355,8 +400,8 @@
             dma((3 * planes,)),
             dma((3 * planes,)),
             dma((3,)),
-            dma((4,)),
-            dma((4,)),
+            dma((3,)),
+            dma((3,)),
             pltpu.SemaphoreType.REGULAR,
             pltpu.SemaphoreType.REGULAR,
         ],

time: 67.7 us -> 66.1 us (0.976)
  the two profiles are of different devices: /device:TPU:1 before, /device:TPU:10 now
where the time goes in v3:
time: 66.1 us; the launch traced here: 66 us
  Pallas kernels  64.7 us (98%)
  other arithmetic  1.3 us (2%)
    pallas_call x1, Pallas kernels, per_device(): pl.pallas_call(functools.partial(kernel, (ny, nz, nx, planes, keep, n)),...  64.7 us

profile of v3, /device:TPU:10, one launch (start us, length us, event | category | flops | bytes accessed | tf_op | source)
XLA Modules:
  0.0 66.0 jit_solution(1982922624482591170)
XLA Ops:
  0.0 64.7 %shard_map.64 = (f32[3,1024,128]{2,1,0:T(8,128)S(1)}, f32[3,1024,128]{2,1,0:T(8,128)S(1)}) custom-call(f32[3,3,192,384]{3,2,1,0:T(8,128)} %v_hbm.1, f32[3,3,192,384]{3,2,1,0:T(8,128)} %w_hbm.1, f32[3,1024,128]{2,1,0:T(8,128)} %bitcast.2, bf16[2,1152,256]{2,1,0:T(8,128)(2,1)} %constant.6.clone.tx_hbm, bf16[2,256,576]{2,1,0:T(8,128)(2,1)} %constant.7.clone.ty_hbm, ...), custom_call_target="tpu_custom_call" | custom-call | tf_op jit(solution)/shard_map/pallas_call | solution.py:379
  64.7 1.3 %sub.3 = f32[3,1024,128]{2,1,0:T(8,128)} subtract(f32[3,1024,128]{2,1,0:T(8,128)S(1)} %get-tuple-element.7, f32[3,1024,128]{2,1,0:T(8,128)S(1)} %get-tuple-element.8) | non-fusion elementwise | flops 393216 | bytes 4718592 | tf_op jit(solution)/shard_map/sub | solution.py:412

commit v4 on v3

--- a/solution.py
+++ b/solution.py
@@ -54,7 +54,7 @@
 
 
 def kernel(
-    dims, v_hbm, w_hbm, m_hbm, tx_hbm, ty_hbm, tz_hbm, out, viscous,
+    dims, v_hbm, w_hbm, m_hbm, tx_hbm, ty_hbm, tz_hbm, out,
     v, w, modes, tx, ty, tz, own, away, arrived, outbox, inbox, spec,
     in_sem, m_sem, t_sem, xs_sem, xr_sem, self_sem, s_sem, r_sem, plane_sem, all_sem,
 ):
@@ -298,7 +298,7 @@
         swap(2 * planes + z).start()
     with jax.named_scope("y2"):
         looped(y_plane, 2)
-    send(1)
+    send(1, near=True)
     keep_own(1).start()
     send(2, by_place=True)
     keep_own(2).start()
@@ -317,13 +317,6 @@
         return waves, ksq, kept
 
     mode_load.wait()
-    with jax.named_scope("viscous"):
-        for q in range(2):
-            _, ksq, _ = waves_of(q)
-            for part in range(2):
-                rows = pl.ds(2 * q + part, keep, stride=4)
-                for c in range(3):
-                    viscous[c, rows, :] = visc * ksq * modes[c, rows, :]
     z_table.wait()
 
     def z_rows(c, q):
@@ -346,7 +339,8 @@
             s = [spec[c, row] for c in range(3)]
             inner = (waves[0] * s[0] + waves[1] * s[1] + waves[2] * s[2]) * scale
             for c in range(3):
-                out[c, pl.ds(row, keep, stride=4), :] = (s[c] - waves[c] * inner) * kept
+                rows = pl.ds(row, keep, stride=4)
+                out[c, rows, :] = (s[c] - waves[c] * inner) * kept - visc * ksq * modes[c, rows, :]
 
     for part, ready in enumerate((((0, 0), (0, 1)), ((1, 0), (1, 1), (2, 0)), ((2, 1),))):
         with jax.named_scope("recv"):
@@ -366,6 +360,18 @@
             all_of(part, s_sem).wait()
 
 
+def leave(held, out, sem):
+    pieces = [(c, pl.ds(h * 512, 512)) for c in range(3) for h in range(2)]
+    copies = [
+        pltpu.make_async_copy(held.at[c, rows], out.at[c, rows], sem.at[i])
+        for i, (c, rows) in enumerate(pieces)
+    ]
+    for copy in copies:
+        copy.start()
+    for copy in copies:
+        copy.wait()
+
+
 def per_device(sizes, velocity, vorticity, velocity_modes):
     ny, nz, nx = sizes
     _, planes, rows, n = velocity.shape
@@ -376,11 +382,11 @@
     dma = pltpu.SemaphoreType.DMA
     whole = jax.ShapeDtypeStruct((3, 4 * keep, half), f32)
     operands = (velocity, vorticity, velocity_modes.reshape(whole.shape), tx, ty, tz)
-    projected, viscous = pl.pallas_call(
+    held = pl.pallas_call(
         functools.partial(kernel, (ny, nz, nx, planes, keep, n)),
-        out_shape=(whole, whole),
+        out_shape=whole,
         in_specs=[pl.BlockSpec(memory_space=pltpu.HBM)] * 6,
-        out_specs=(pl.BlockSpec(memory_space=pltpu.VMEM),) * 2,
+        out_specs=pl.BlockSpec(memory_space=pltpu.VMEM),
         scratch_shapes=[
             pltpu.VMEM((3, planes, rows, n), f32),
             pltpu.VMEM((3, planes, rows, n), f32),
@@ -409,7 +415,15 @@
             collective_id=0, has_side_effects=True, vmem_limit_bytes=30 << 20
         ),
     )(*(pltpu.with_memory_space_constraint(x, pltpu.HBM) for x in operands))
-    return (projected - viscous).reshape(velocity_modes.shape)
+    out = pl.pallas_call(
+        leave,
+        out_shape=whole,
+        in_specs=[pl.BlockSpec(memory_space=pltpu.VMEM)],
+        out_specs=pl.BlockSpec(memory_space=pltpu.HBM),
+        scratch_shapes=[dma((6,))],
+        compiler_params=pltpu.CompilerParams(vmem_limit_bytes=4 << 20),
+    )(held)
+    return out.reshape(velocity_modes.shape)
 
 
 def solution(mesh):

time: 66.1 us -> 66 us (level)
  other arithmetic: 1.3 us -> 0 us
  Pallas kernels: 64.7 us -> 65.9 us
    sub x1 -> x0, other arithmetic: 1.3 us -> none  [per_device(): return (projected - viscous).reshape(velocity_modes.shape)]
    pallas_call x0 -> x1, Pallas kernels: none -> 1.19 us  [per_device(): pl.pallas_call(leave, out_shape=whole, in_specs=[pl.BlockSpec(memory_spac...]
where the time goes in v4:
time: 66 us; the launch traced here: 65.9 us
  Pallas kernels  65.9 us (100%)
    pallas_call x1, Pallas kernels, per_device(): pl.pallas_call(functools.partial(kernel, (ny, nz, nx, planes, keep, n)),...  64.7 us

profile of v4, /device:TPU:10, one launch (start us, length us, event | category | flops | bytes accessed | tf_op | source)
XLA Modules:
  0.0 65.9 jit_solution(14881314885123565189)
XLA Ops:
  0.0 64.7 %shard_map.64.held = f32[3,1024,128]{2,1,0:T(8,128)S(1)} custom-call(f32[3,3,192,384]{3,2,1,0:T(8,128)} %v_hbm.1, f32[3,3,192,384]{3,2,1,0:T(8,128)} %w_hbm.1, f32[3,1024,128]{2,1,0:T(8,128)} %bitcast.2, bf16[2,1152,256]{2,1,0:T(8,128)(2,1)} %constant.6.clone.tx_hbm, bf16[2,256,576]{2,1,0:T(8,128)(2,1)} %constant.7.clone.ty_hbm, ...), custom_call_target="tpu_custom_call" | custom-call | tf_op jit(solution)/shard_map/pallas_call | solution.py:385
  64.7 1.2 %shard_map.65 = f32[3,1024,128]{2,1,0:T(8,128)} custom-call(f32[3,1024,128]{2,1,0:T(8,128)S(1)} %shard_map.64.held), custom_call_target="tpu_custom_call" | custom-call | tf_op jit(solution)/shard_map/pallas_call | solution.py:418

commit v5 on v3

--- a/solution.py
+++ b/solution.py
@@ -283,7 +283,7 @@
         send(0, z * 4, 4, first=plane, near=True)
     with jax.named_scope("all"):
         pl.semaphore_wait(all_sem, ny - 1)
-    send(0, last=plane, near=True)
+    send(0, last=plane)
     keep_own(0).start()
     for copy in fields[planes]:
         copy.wait()
@@ -298,7 +298,7 @@
         swap(2 * planes + z).start()
     with jax.named_scope("y2"):
         looped(y_plane, 2)
-    send(1)
+    send(1, near=True)
     keep_own(1).start()
     send(2, by_place=True)
     keep_own(2).start()

time: 66.1 us -> 66.1 us (level)
  no operation moved by 1% of the time
where the time goes in v5:
time: 66.1 us; the launch traced here: 66 us
  Pallas kernels  64.7 us (98%)
  other arithmetic  1.3 us (2%)
    pallas_call x1, Pallas kernels, per_device(): pl.pallas_call(functools.partial(kernel, (ny, nz, nx, planes, keep, n)),...  64.7 us

profile of v5, /device:TPU:10, one launch (start us, length us, event | category | flops | bytes accessed | tf_op | source)
XLA Modules:
  0.0 66.0 jit_solution(4171577760649238133)
XLA Ops:
  0.0 64.7 %shard_map.64 = (f32[3,1024,128]{2,1,0:T(8,128)S(1)}, f32[3,1024,128]{2,1,0:T(8,128)S(1)}) custom-call(f32[3,3,192,384]{3,2,1,0:T(8,128)} %v_hbm.1, f32[3,3,192,384]{3,2,1,0:T(8,128)} %w_hbm.1, f32[3,1024,128]{2,1,0:T(8,128)} %bitcast.2, bf16[2,1152,256]{2,1,0:T(8,128)(2,1)} %constant.6.clone.tx_hbm, bf16[2,256,576]{2,1,0:T(8,128)(2,1)} %constant.7.clone.ty_hbm, ...), custom_call_target="tpu_custom_call" | custom-call | tf_op jit(solution)/shard_map/pallas_call | solution.py:379
  64.7 1.3 %sub.3 = f32[3,1024,128]{2,1,0:T(8,128)} subtract(f32[3,1024,128]{2,1,0:T(8,128)S(1)} %get-tuple-element.7, f32[3,1024,128]{2,1,0:T(8,128)S(1)} %get-tuple-element.8) | non-fusion elementwise | flops 393216 | bytes 4718592 | tf_op jit(solution)/shard_map/sub | solution.py:412
